TPU v7x, 128 devices: a whole 4x4x4 slice. The times are simulated.
128 devices in a mesh: row: 16 (over y, z), col: 8 (over x, core).
Axes of the slice: x: 4, y: 4, z: 4, core: 2. Of those that a mesh axis runs over, the one named last changes fastest.
Arguments:
- matrix: float32 [4096, 4096], P('row', 'col'), may hold values from -0.92 to 1.92, as said below
Outputs:
- inverse: float32 [4096, 4096], P('row', 'col')
- residual_norms: float32 [4], replicated
Inputs may be any that keep to these rules, and one draw needn't show every extreme that they name: matrix is exactly symmetric and positive definite; all its eigenvalues lie between 0.08 and 1.92.
All inputs are finite; a program needn't handle non-finite values.
Results may differ from a plain program's by a relative error of at most 0.0017.
The roundings to bfloat16 on the way count: a program that leaves them out, or rounds other values in their place, can miss the bound.
Values may be sent and summed in bfloat16 or wider, within the bound.
A program may use at most 64 MiB of HBM per device.

v0:
```python
import functools

import jax
import jax.numpy as jnp
from jax import lax
from jax.sharding import Mesh
from jax.sharding import PartitionSpec as P

N = 4096
ITERS = 4
ROW = ("row_0", "row_1")
COL = ("col_0", "col_1")
ROW_COL = ("row_0", "row_1", "col_0", "col_1")


def over_axes(x, axes):
    return functools.reduce(lax.psum, axes, x)


def laid_out(pieces, dim):
    dims = list(pieces.shape[1:])
    dims[dim] *= pieces.shape[0]
    return jnp.moveaxis(pieces, 0, dim).reshape(dims)


def sent_to_all(x, axis):
    count = lax.axis_size(axis)
    return lax.all_to_all(jnp.broadcast_to(x[None], (count, *x.shape)), axis, 0, 0, tiled=True)


def collect(x, axis, dim):
    return laid_out(sent_to_all(x, axis), dim)


def shards(matrix):
    row_count, col_count = matrix.shape
    row_index = lax.axis_index(ROW)
    col_index = lax.axis_index(COL)
    sq_total = over_axes(jnp.sum(matrix * matrix), ROW_COL)
    start_scale = jnp.sqrt(jnp.float32(N)) / jnp.sqrt(sq_total)
    global_rows = row_index * row_count + lax.broadcasted_iota(jnp.int32, (row_count, col_count), 0)
    global_cols = col_index * col_count + lax.broadcasted_iota(jnp.int32, (row_count, col_count), 1)
    eye_block = (global_rows == global_cols).astype(jnp.float32)
    mat_low = matrix.astype(jnp.bfloat16)
    panel_rows = collect(mat_low, COL, 1)
    current = start_scale * eye_block
    partial_list = []
    for iteration in range(ITERS):
        cur_low = current.astype(jnp.bfloat16)
        product = jnp.dot(
            panel_rows,
            lax.all_gather(cur_low, ROW, axis=0, tiled=True),
            preferred_element_type=jnp.float32,
        )
        residual = eye_block - product
        local_sum = jnp.sum(residual * residual)
        partial_list.append(local_sum)
        shift_low = (eye_block + residual).astype(jnp.bfloat16)
        iterate_rows = collect(cur_low, COL, 1)
        current = jnp.dot(
            iterate_rows,
            lax.all_gather(shift_low, ROW, axis=0, tiled=True),
            preferred_element_type=jnp.float32,
        )
    summed = over_axes(jnp.stack(partial_list), ROW_COL)
    residual_norms = jnp.sqrt(summed / N)
    return (current, residual_norms)


def solution(mesh):
    split = Mesh(mesh.devices.reshape(4, 4, 4, 2), ("row_0", "row_1", "col_0", "col_1"))
    placed = (P(ROW, COL),)
    return jax.shard_map(
        shards, mesh=split, in_specs=placed, out_specs=(P(ROW, COL), P()), check_vma=False
    )
```

profile of v0, /device:TPU:59, one launch (start us, length us, event | category | flops | bytes accessed | tf_op | source)
XLA Modules:
  0.0 521.1 jit_solution(16021957152768351581)
XLA Ops:
  7.2 2.0 fusion.5
  9.2 6.4 %psum.56 = f32[]{:T(128)} all-reduce(f32[]{:T(128)} %get-tuple-element.11), channel_id=1, replica_groups=mesh['row_0'=4,'row_1'=4,'col_0'=4,'col_1'=2] {'row_0'}, use_global_device_ids=true, to_apply=%region_1.0 | all-reduce | flops 1 | bytes 8 | tf_op jit(solution)/shard_map/psum | solution.py:17
  15.5 7.6 %psum.57 = f32[]{:T(128)} all-reduce(f32[]{:T(128)} %psum.56), channel_id=1, replica_groups=mesh['row_0'=4,'row_1'=4,'col_0'=4,'col_1'=2] {'row_1'}, use_global_device_ids=true, to_apply=%region_2.0 | all-reduce | flops 1 | bytes 8 | tf_op jit(solution)/shard_map/psum | solution.py:17
  23.2 7.2 %psum.58 = f32[]{:T(128)} all-reduce(f32[]{:T(128)} %psum.57), channel_id=1, replica_groups=mesh['row_0'=4,'row_1'=4,'col_0'=4,'col_1'=2] {'col_0'}, use_global_device_ids=true, to_apply=%region_3.0 | all-reduce | flops 1 | bytes 8 | tf_op jit(solution)/shard_map/psum | solution.py:17
  30.4 9.2 %psum.59 = f32[]{:T(128)} all-reduce(f32[]{:T(128)} %psum.58), channel_id=1, replica_groups=mesh['row_0'=4,'row_1'=4,'col_0'=4,'col_1'=2] {'col_1'}, use_global_device_ids=true, to_apply=%region_4.0 | all-reduce | flops 1 | bytes 8 | tf_op jit(solution)/shard_map/psum | solution.py:17
  41.5 30.1 %all_to_all.25 = bf16[8,256,512]{1,2,0:T(8,128)(2,1)S(1)} all-to-all(bf16[8,256,512]{1,2,0:T(8,128)(2,1)S(1)} %broadcast_in_dim.11), channel_id=1, replica_groups=mesh['row_0'=4,'row_1'=4,'col_0'=4,'col_1'=2] {'col_0','col_1'}, dimensions={0} | all-to-all | bytes 4194304 | tf_op jit(solution)/shard_map/all_to_all | solution.py:28
  71.6 25.1 %all-gather.9.cloned.1.call-done = bf16[4096,512]{0,1:T(8,128)(2,1)} async-done(((bf16[256,512]{0,1:T(8,128)(2,1)}), bf16[4096,512]{0,1:T(8,128)(2,1)}) %all-gather.9.cloned.1.call-update) | async-done | bytes 4194320 | tf_op jit(solution)/shard_map/all_gather | solution.py:52
  96.7 4.8 multiply_reduce_fusion.3
  101.8 31.7 %all_to_all.26 = bf16[8,256,512]{1,2,0:T(8,128)(2,1)} all-to-all(bf16[8,256,512]{1,2,0:T(8,128)(2,1)S(1)} %broadcast_in_dim.10), channel_id=1, replica_groups=mesh['row_0'=4,'row_1'=4,'col_0'=4,'col_1'=2] {'col_0','col_1'}, dimensions={0} | all-to-all | bytes 4194304 | tf_op jit(solution)/shard_map/all_to_all | solution.py:28
  133.5 24.5 %all-gather.11.cloned.1.call-done = bf16[4096,512]{0,1:T(8,128)(2,1)} async-done(((bf16[256,512]{0,1:T(8,128)(2,1)}), bf16[4096,512]{0,1:T(8,128)(2,1)}) %all-gather.11.cloned.1.call-update) | async-done | bytes 4194320 | tf_op jit(solution)/shard_map/all_gather | solution.py:62
  158.0 4.8 convolution_convert_fusion.2
  162.9 52.4 %all-gather.13.cloned.1.call-done = bf16[4096,512]{1,0:T(8,128)(2,1)} async-done(((bf16[256,512]{1,0:T(8,128)(2,1)}), bf16[4096,512]{1,0:T(8,128)(2,1)}) %all-gather.13.cloned.1.call-update) | async-done | bytes 4194320 | tf_op jit(solution)/shard_map/all_gather | solution.py:52
  215.2 4.8 multiply_reduce_fusion.2
  220.4 30.5 %all_to_all.27 = bf16[8,256,512]{1,2,0:T(8,128)(2,1)} all-to-all(bf16[8,256,512]{1,2,0:T(8,128)(2,1)S(1)} %broadcast_in_dim.12), channel_id=1, replica_groups=mesh['row_0'=4,'row_1'=4,'col_0'=4,'col_1'=2] {'col_0','col_1'}, dimensions={0} | all-to-all | bytes 4194304 | tf_op jit(solution)/shard_map/all_to_all | solution.py:28
  250.9 24.3 %all-gather.15.cloned.1.call-done = bf16[4096,512]{0,1:T(8,128)(2,1)} async-done(((bf16[256,512]{0,1:T(8,128)(2,1)}), bf16[4096,512]{0,1:T(8,128)(2,1)}) %all-gather.15.cloned.1.call-update) | async-done | bytes 4194320 | tf_op jit(solution)/shard_map/all_gather | solution.py:62
  275.3 4.8 convolution_convert_fusion.1
  280.2 52.4 %all-gather.17.cloned.1.call-done = bf16[4096,512]{1,0:T(8,128)(2,1)} async-done(((bf16[256,512]{1,0:T(8,128)(2,1)}), bf16[4096,512]{1,0:T(8,128)(2,1)}) %all-gather.17.cloned.1.call-update) | async-done | bytes 4194320 | tf_op jit(solution)/shard_map/all_gather | solution.py:52
  332.6 4.9 multiply_reduce_fusion.1
  337.8 30.5 %all_to_all.28 = bf16[8,256,512]{1,2,0:T(8,128)(2,1)} all-to-all(bf16[8,256,512]{1,2,0:T(8,128)(2,1)S(1)} %broadcast_in_dim.13), channel_id=1, replica_groups=mesh['row_0'=4,'row_1'=4,'col_0'=4,'col_1'=2] {'col_0','col_1'}, dimensions={0} | all-to-all | bytes 4194304 | tf_op jit(solution)/shard_map/all_to_all | solution.py:28
  368.3 24.3 %all-gather.19.cloned.1.call-done = bf16[4096,512]{0,1:T(8,128)(2,1)} async-done(((bf16[256,512]{0,1:T(8,128)(2,1)}), bf16[4096,512]{0,1:T(8,128)(2,1)}) %all-gather.19.cloned.1.call-update) | async-done | bytes 4194320 | tf_op jit(solution)/shard_map/all_gather | solution.py:62
  392.6 4.8 convolution_convert_fusion
  397.5 52.4 %all-gather.21.cloned.1.call-done = bf16[4096,512]{1,0:T(8,128)(2,1)} async-done(((bf16[256,512]{1,0:T(8,128)(2,1)}), bf16[4096,512]{1,0:T(8,128)(2,1)}) %all-gather.21.cloned.1.call-update) | async-done | bytes 4194320 | tf_op jit(solution)/shard_map/all_gather | solution.py:52
  449.9 4.8 multiply_reduce_fusion
  454.9 1.5 broadcast_in_dim.14
  456.4 5.3 %all-to-all-start.4 = ((bf16[8,256,512]{1,2,0:T(8,128)(2,1)}), bf16[8,256,512]{1,2,0:T(8,128)(2,1)S(1)}, u32[]{:S(2)}, u32[]{:S(2)}) async-start(bf16[8,256,512]{1,2,0:T(8,128)(2,1)} %broadcast_in_dim.14), calls=%async_computation.4 | async-start | bytes 4194304 | tf_op jit(solution)/shard_map/all_to_all | solution.py:28
  461.6 2.5 pad_maximum_fusion
  464.2 6.8 %psum.60 = f32[4]{0:T(128)S(1)} all-reduce(f32[4]{0:T(128)S(1)} %pad_maximum_fusion), channel_id=1, replica_groups=mesh['row_0'=4,'row_1'=4,'col_0'=4,'col_1'=2] {'row_0'}, use_global_device_ids=true, to_apply=%region_9.0 | all-reduce | flops 4 | bytes 32 | tf_op jit(solution)/shard_map/psum | solution.py:17
  471.0 7.2 %psum.61 = f32[4]{0:T(128)S(1)} all-reduce(f32[4]{0:T(128)S(1)} %psum.60), channel_id=1, replica_groups=mesh['row_0'=4,'row_1'=4,'col_0'=4,'col_1'=2] {'row_1'}, use_global_device_ids=true, to_apply=%region_10.0 | all-reduce | flops 4 | bytes 32 | tf_op jit(solution)/shard_map/psum | solution.py:17
  478.2 9.3 %psum.62 = f32[4]{0:T(128)S(1)} all-reduce(f32[4]{0:T(128)S(1)} %psum.61), channel_id=1, replica_groups=mesh['row_0'=4,'row_1'=4,'col_0'=4,'col_1'=2] {'col_0'}, use_global_device_ids=true, to_apply=%region_11.0 | all-reduce | flops 4 | bytes 32 | tf_op jit(solution)/shard_map/psum | solution.py:17
  487.5 5.1 psum.63
  493.1 16.8 %all-gather.23.cloned.1.call-done = bf16[4096,512]{0,1:T(8,128)(2,1)} async-done(((bf16[256,512]{0,1:T(8,128)(2,1)}), bf16[4096,512]{0,1:T(8,128)(2,1)}) %all-gather.23.cloned.1.call-update) | async-done | bytes 4194320 | tf_op jit(solution)/shard_map/all_gather | solution.py:62
  510.0 4.3 fusion.6
  (37 shorter events, 2.9 us)
Async XLA Ops:
  7.2 89.6 %all-gather.9.cloned.1.call-start = ((), (), s32[]{:S(2)}) async-start(), calls=%async_computation.5 | async-start | bytes 4456448 | tf_op jit(solution)/shard_map/all_gather | solution.py:52
  41.1 116.8 %all-gather.11.cloned.1.call-start = ((), (), s32[]{:S(2)}) async-start(), calls=%async_computation.6 | async-start | bytes 4456448 | tf_op jit(solution)/shard_map/all_gather | solution.py:62
  96.7 4.9 copy-start
  101.6 113.6 %all-gather.13.cloned.1.call-start = ((), (), s32[]{:S(2)}) async-start(), calls=%async_computation.7 | async-start | bytes 4456448 | tf_op jit(solution)/shard_map/all_gather | solution.py:52
  162.8 57.3 %copy-start.2 = (bf16[256,512]{1,0:T(8,128)(2,1)S(1)}, bf16[256,512]{1,0:T(8,128)(2,1)}, u32[]{:S(2)}) copy-start(bf16[256,512]{1,0:T(8,128)(2,1)} %convolution_convert_fusion.2) | copy-start | bytes 786436
  162.8 112.4 %all-gather.15.cloned.1.call-start = ((), (), s32[]{:S(2)}) async-start(), calls=%async_computation.8 | async-start | bytes 4456448 | tf_op jit(solution)/shard_map/all_gather | solution.py:62
  220.1 112.5 %all-gather.17.cloned.1.call-start = ((), (), s32[]{:S(2)}) async-start(), calls=%async_computation.9 | async-start | bytes 4456448 | tf_op jit(solution)/shard_map/all_gather | solution.py:52
  280.1 57.4 %copy-start.3 = (bf16[256,512]{1,0:T(8,128)(2,1)S(1)}, bf16[256,512]{1,0:T(8,128)(2,1)}, u32[]{:S(2)}) copy-start(bf16[256,512]{1,0:T(8,128)(2,1)} %convolution_convert_fusion.1) | copy-start | bytes 786436
  280.1 112.5 %all-gather.19.cloned.1.call-start = ((), (), s32[]{:S(2)}) async-start(), calls=%async_computation.10 | async-start | bytes 4456448 | tf_op jit(solution)/shard_map/all_gather | solution.py:62
  337.4 112.5 %all-gather.21.cloned.1.call-start = ((), (), s32[]{:S(2)}) async-start(), calls=%async_computation.11 | async-start | bytes 4456448 | tf_op jit(solution)/shard_map/all_gather | solution.py:52
  397.5 57.3 %copy-start.1 = (bf16[256,512]{1,0:T(8,128)(2,1)S(1)}, bf16[256,512]{1,0:T(8,128)(2,1)}, u32[]{:S(2)}) copy-start(bf16[256,512]{1,0:T(8,128)(2,1)} %convolution_convert_fusion) | copy-start | bytes 786436
  397.5 112.5 %all-gather.23.cloned.1.call-start = ((), (), s32[]{:S(2)}) async-start(), calls=%async_computation.12 | async-start | bytes 4456448 | tf_op jit(solution)/shard_map/all_gather | solution.py:62
  456.4 36.8 %all-to-all-start.4 = ((bf16[8,256,512]{1,2,0:T(8,128)(2,1)}), bf16[8,256,512]{1,2,0:T(8,128)(2,1)S(1)}, u32[]{:S(2)}, u32[]{:S(2)}) async-start(bf16[8,256,512]{1,2,0:T(8,128)(2,1)} %broadcast_in_dim.14), calls=%async_computation.4 | async-start | bytes 4194304 | tf_op jit(solution)/shard_map/all_to_all | solution.py:28
Sparse Core Ops, SparseCore 0:
  41.3 55.4 all-gather.8
  101.7 56.1 all-gather.10
  162.9 52.2 all-gather.12
  220.2 55.0 all-gather.14
  280.2 52.2 all-gather.16
  337.6 55.0 all-gather.18
  397.6 52.2 all-gather.20
  454.9 55.0 all-gather.22
where the time goes:
time: 526 us; the launch traced here: 521 us
  waiting for transfers between devices  272 us (52%)
  blocking collectives  182 us (35%)
  matrix products  38.1 us (7%)
  between operations  15 us (3%)
  other arithmetic  5.89 us (1%)
  starting transfers between devices  5.58 us (1%)
    all_gather x4, waiting for transfers between devices, shards(): lax.all_gather(cur_low, ROW, axis=0, tiled=True)  182 us
    all_to_all x4, blocking collectives, sent_to_all(): lax.all_to_all(jnp.broadcast_to(x[None], (count, *x.shape)), axis, 0, 0,...  123 us
    all_gather x4, waiting for transfers between devices, shards(): lax.all_gather(shift_low, ROW, axis=0, tiled=True)  90 us
    psum x8, blocking collectives, over_axes(): return functools.reduce(lax.psum, axes, x)  58.8 us
    dot_general x4, matrix products, shards(): jnp.dot(panel_rows, lax.all_gather(cur_low, ROW, axis=0, tiled=True), pre...  19.3 us
    dot_general x4, matrix products, shards(): jnp.dot(iterate_rows, lax.all_gather(shift_low, ROW, axis=0, tiled=True),...  18.7 us
  transfers between devices with their start and end apart: 9, of which 8 were waited for; matrix products, arithmetic and copies ran while one was open for 1% of the time, Pallas kernels for 0%

commit v1 on v0

--- a/solution.py
+++ b/solution.py
@@ -32,31 +32,42 @@
     return laid_out(sent_to_all(x, axis), dim)
 
 
+def eye_at(shape, row0, col0):
+    rows = row0 + lax.broadcasted_iota(jnp.int32, shape, 0)
+    cols = col0 + lax.broadcasted_iota(jnp.int32, shape, 1)
+    return (rows == cols).astype(jnp.float32)
+
+
 def shards(matrix):
     row_count, col_count = matrix.shape
-    row_index = lax.axis_index(ROW)
-    col_index = lax.axis_index(COL)
+    row0 = lax.axis_index(ROW) * row_count
+    col0 = lax.axis_index(COL) * col_count
     sq_total = over_axes(jnp.sum(matrix * matrix), ROW_COL)
     start_scale = jnp.sqrt(jnp.float32(N)) / jnp.sqrt(sq_total)
-    global_rows = row_index * row_count + lax.broadcasted_iota(jnp.int32, (row_count, col_count), 0)
-    global_cols = col_index * col_count + lax.broadcasted_iota(jnp.int32, (row_count, col_count), 1)
-    eye_block = (global_rows == global_cols).astype(jnp.float32)
+    scale_low = start_scale.astype(jnp.bfloat16).astype(jnp.float32)
+    eye_block = eye_at(matrix.shape, row0, col0)
     mat_low = matrix.astype(jnp.bfloat16)
     panel_rows = collect(mat_low, COL, 1)
-    current = start_scale * eye_block
-    partial_list = []
-    for iteration in range(ITERS):
-        cur_low = current.astype(jnp.bfloat16)
-        product = jnp.dot(
-            panel_rows,
-            lax.all_gather(cur_low, ROW, axis=0, tiled=True),
-            preferred_element_type=jnp.float32,
-        )
+    panel_cols = lax.all_gather(mat_low, ROW, axis=0, tiled=True)
+
+    def first(mat, eye):
+        residual = eye - scale_low * mat.astype(jnp.float32)
+        shift_low = (eye + residual).astype(jnp.bfloat16)
+        return residual, (scale_low * shift_low.astype(jnp.float32)).astype(jnp.bfloat16)
+
+    residual, _ = first(mat_low, eye_block)
+    partial_list = [jnp.sum(residual * residual)]
+    _, iterate_rows = first(panel_rows, eye_at(panel_rows.shape, row0, 0))
+    _, iterate_cols = first(panel_cols, eye_at(panel_cols.shape, 0, col0))
+    for iteration in range(1, ITERS):
+        if iteration > 1:
+            cur_low = current.astype(jnp.bfloat16)
+            iterate_cols = lax.all_gather(cur_low, ROW, axis=0, tiled=True)
+            iterate_rows = collect(cur_low, COL, 1)
+        product = jnp.dot(panel_rows, iterate_cols, preferred_element_type=jnp.float32)
         residual = eye_block - product
-        local_sum = jnp.sum(residual * residual)
-        partial_list.append(local_sum)
+        partial_list.append(jnp.sum(residual * residual))
         shift_low = (eye_block + residual).astype(jnp.bfloat16)
-        iterate_rows = collect(cur_low, COL, 1)
         current = jnp.dot(
             iterate_rows,
             lax.all_gather(shift_low, ROW, axis=0, tiled=True),

time: 526 us -> 379 us (0.72)
  blocking collectives: 182 us -> 89.3 us
  waiting for transfers between devices: 272 us -> 217 us
  matrix products: 38.1 us -> 30 us
  local copies, waits for them, and re-layouts: 2.57 us -> 8.82 us
    all_to_all x4 -> x1, blocking collectives: 123 us -> 30.5 us  [sent_to_all(): lax.all_to_all(jnp.broadcast_to(x[None], (count, *x.shape)), axis, 0, 0,...]
    all_gather x4 -> x3, waiting for transfers between devices: 182 us -> 120 us  [the longest x2 105 us: shards(): iterate_cols = lax.all_gather(cur_low, ROW, axis=0, tiled=True)]
    all_gather x4 -> x3, waiting for transfers between devices: 90 us -> 97.5 us  [shards(): lax.all_gather(shift_low, ROW, axis=0, tiled=True)]
    dot_general x4 -> x3, matrix products: 18.7 us -> 13.5 us  [shards(): jnp.dot(iterate_rows, lax.all_gather(shift_low, ROW, axis=0, tiled=True),...]
    dot_general x4 -> x3, matrix products: 19.3 us -> 16.5 us  [shards(): jnp.dot(panel_rows, iterate_cols, preferred_element_type=jnp.float32)]
  transfers between devices with their start and end apart: 9 -> 8, of which waited for: 8 -> 6; matrix products, arithmetic and copies ran while one was open for 1% -> 3% of each run, Pallas kernels for 0% -> 0%
where the time goes in v1:
time: 379 us; the launch traced here: 375 us
  waiting for transfers between devices  217 us (57%)
  blocking collectives  89.3 us (24%)
  matrix products  30 us (8%)
  between operations  14.9 us (4%)
  starting transfers between devices  10.6 us (3%)
  local copies, waits for them, and re-layouts  8.82 us (2%)
  other arithmetic  3.81 us (1%)
    all_gather x2, waiting for transfers between devices, shards(): iterate_cols = lax.all_gather(cur_low, ROW, axis=0, tiled=True)  105 us
    all_gather x3, waiting for transfers between devices, shards(): lax.all_gather(shift_low, ROW, axis=0, tiled=True)  97.5 us
    psum x8, blocking collectives, over_axes(): return functools.reduce(lax.psum, axes, x)  58.8 us
    all_to_all x1, blocking collectives, sent_to_all(): lax.all_to_all(jnp.broadcast_to(x[None], (count, *x.shape)), axis, 0, 0,...  30.5 us
    dot_general x3, matrix products, shards(): jnp.dot(panel_rows, iterate_cols, preferred_element_type=jnp.float32)  16.5 us
    all_gather x1, waiting for transfers between devices, shards(): panel_cols = lax.all_gather(mat_low, ROW, axis=0, tiled=True)  15.2 us
    dot_general x3, matrix products, shards(): jnp.dot(iterate_rows, lax.all_gather(shift_low, ROW, axis=0, tiled=True),...  13.5 us
    all_to_all x2, starting transfers between devices, sent_to_all(): lax.all_to_all(jnp.broadcast_to(x[None], (count, *x.shape)), axis, 0, 0,...  10.4 us
  transfers between devices with their start and end apart: 8, of which 6 were waited for; matrix products, arithmetic and copies ran while one was open for 3% of the time, Pallas kernels for 0%

profile of v1, /device:TPU:59, one launch (start us, length us, event | category | flops | bytes accessed | tf_op | source)
XLA Modules:
  0.0 374.9 jit_solution(14073565406536104907)
XLA Ops:
  7.2 1.9 copy.13
  9.2 1.1 copy.14
  10.3 1.5 broadcast_in_dim.6
  11.8 5.1 %all-to-all-start = ((bf16[8,256,512]{2,1,0:T(8,128)(2,1)}), bf16[8,256,512]{2,1,0:T(8,128)(2,1)S(1)}, u32[]{:S(2)}, u32[]{:S(2)}) async-start(bf16[8,256,512]{2,1,0:T(8,128)(2,1)} %broadcast_in_dim.6), calls=%async_computation | async-start | bytes 4194304 | tf_op jit(solution)/shard_map/all_to_all | solution.py:28
  16.9 0.7 multiply_reduce_fusion.3
  17.6 6.5 %psum.56 = f32[]{:T(128)} all-reduce(f32[]{:T(128)} %multiply_reduce_fusion.3), channel_id=1, replica_groups=mesh['row_0'=4,'row_1'=4,'col_0'=4,'col_1'=2] {'row_0'}, use_global_device_ids=true, to_apply=%region_1.0 | all-reduce | flops 1 | bytes 8 | tf_op jit(solution)/shard_map/psum | solution.py:17
  24.1 7.9 %psum.57 = f32[]{:T(128)} all-reduce(f32[]{:T(128)} %psum.56), channel_id=1, replica_groups=mesh['row_0'=4,'row_1'=4,'col_0'=4,'col_1'=2] {'row_1'}, use_global_device_ids=true, to_apply=%region_2.0 | all-reduce | flops 1 | bytes 8 | tf_op jit(solution)/shard_map/psum | solution.py:17
  32.1 11.3 %psum.58 = f32[]{:T(128)} all-reduce(f32[]{:T(128)} %psum.57), channel_id=1, replica_groups=mesh['row_0'=4,'row_1'=4,'col_0'=4,'col_1'=2] {'col_0'}, use_global_device_ids=true, to_apply=%region_3.0 | all-reduce | flops 1 | bytes 8 | tf_op jit(solution)/shard_map/psum | solution.py:17
  43.3 4.7 %psum.59 = f32[]{:T(128)} all-reduce(f32[]{:T(128)} %psum.58), channel_id=1, replica_groups=mesh['row_0'=4,'row_1'=4,'col_0'=4,'col_1'=2] {'col_1'}, use_global_device_ids=true, to_apply=%region_4.0 | all-reduce | flops 1 | bytes 8 | tf_op jit(solution)/shard_map/psum | solution.py:17
  48.8 2.4 copy.15
  51.2 15.2 %all-gather.7.cloned.1.call-done = bf16[4096,512]{0,1:T(8,128)(2,1)} async-done(((bf16[256,512]{0,1:T(8,128)(2,1)}), bf16[4096,512]{0,1:T(8,128)(2,1)}) %all-gather.7.cloned.1.call-update) | async-done | bytes 4194320 | tf_op jit(solution)/shard_map/all_gather | solution.py:51
  66.3 6.8 %multiply_reduce_fusion.2 = (f32[]{:T(128)}, bf16[256,512]{0,1:T(8,128)(2,1)}) fusion(s32[512]{0:T(512)S(1)} %iota_add_fusion, s32[256]{0:T(256)S(1)} %iota_add_fusion.1, bf16[256,4096]{0,1:T(8,128)(2,1)} %bitcast.35, bf16[4096,512]{0,1:T(8,128)(2,1)} %all-gather.7.cloned.1.call-done, f32[]{:T(128)S(6)} %convert_element_type.61), kind=kOutput, calls=%fused_computation.33 | convolution fusion | flops 1095630848 | bytes 6556680 | tf_op jit(solution)/shard_map/dot_general | solution.py:67
  73.2 56.3 %all-gather.9.cloned.1.call-done = bf16[4096,512]{0,1:T(8,128)(2,1)} async-done(((bf16[256,512]{0,1:T(8,128)(2,1)}), bf16[4096,512]{0,1:T(8,128)(2,1)}) %all-gather.9.cloned.1.call-update) | async-done | bytes 4194320 | tf_op jit(solution)/shard_map/all_gather | solution.py:73
  129.5 4.4 %fusion.11 = bf16[256,512]{1,0:T(8,128)(2,1)} fusion(bf16[4096,512]{0,1:T(8,128)(2,1)} %all-gather.9.cloned.1.call-done, bf16[256,4096]{0,1:T(8,128)(2,1)S(1)} %bitcast.36, s32[256]{0:T(256)S(1)} %iota_add_fusion.1, f32[]{:T(128)S(6)} %convert_element_type.61), kind=kOutput, calls=%fused_computation.25 | convolution fusion | flops 1084358656 | bytes 6554628 | tf_op jit(solution)/shard_map/dot_general | solution.py:71
  133.9 52.4 %all-gather.11.cloned.1.call-done = bf16[4096,512]{1,0:T(8,128)(2,1)} async-done(((bf16[256,512]{1,0:T(8,128)(2,1)}), bf16[4096,512]{1,0:T(8,128)(2,1)}) %all-gather.11.cloned.1.call-update) | async-done | bytes 4194320 | tf_op jit(solution)/shard_map/all_gather | solution.py:65
  186.3 4.8 %multiply_reduce_fusion.1 = (f32[]{:T(128)}, bf16[256,512]{0,1:T(8,128)(2,1)}) fusion(s32[512]{0:T(512)S(1)} %iota_add_fusion, s32[256]{0:T(256)S(1)} %iota_add_fusion.1, bf16[4096,512]{1,0:T(8,128)(2,1)} %all-gather.11.cloned.1.call-done, bf16[256,4096]{0,1:T(8,128)(2,1)S(1)} %bitcast.37), kind=kOutput, calls=%fused_computation.32 | convolution fusion | flops 1074659328 | bytes 6556676 | tf_op jit(solution)/shard_map/dot_general | solution.py:67
  191.4 0.1 broadcast_in_dim.7
  191.5 30.5 %all_to_all.15 = bf16[8,256,512]{1,2,0:T(8,128)(2,1)} all-to-all(bf16[8,256,512]{1,2,0:T(8,128)(2,1)S(1)} %broadcast_in_dim.7), channel_id=1, replica_groups=mesh['row_0'=4,'row_1'=4,'col_0'=4,'col_1'=2] {'col_0','col_1'}, dimensions={0} | all-to-all | bytes 4194304 | tf_op jit(solution)/shard_map/all_to_all | solution.py:28
  222.0 24.3 %all-gather.13.cloned.1.call-done = bf16[4096,512]{0,1:T(8,128)(2,1)} async-done(((bf16[256,512]{0,1:T(8,128)(2,1)}), bf16[4096,512]{0,1:T(8,128)(2,1)}) %all-gather.13.cloned.1.call-update) | async-done | bytes 4194320 | tf_op jit(solution)/shard_map/all_gather | solution.py:73
  246.3 4.8 %convolution_convert_fusion = bf16[256,512]{1,0:T(8,128)(2,1)} fusion(bf16[256,4096]{0,1:T(8,128)(2,1)} %bitcast.40, bf16[4096,512]{0,1:T(8,128)(2,1)} %all-gather.13.cloned.1.call-done), kind=kOutput, calls=%fused_computation.24 | convolution fusion | flops 1073872896 | bytes 6553600 | tf_op jit(solution)/shard_map/dot_general | solution.py:71
  251.3 52.4 %all-gather.15.cloned.1.call-done = bf16[4096,512]{1,0:T(8,128)(2,1)} async-done(((bf16[256,512]{1,0:T(8,128)(2,1)}), bf16[4096,512]{1,0:T(8,128)(2,1)}) %all-gather.15.cloned.1.call-update) | async-done | bytes 4194320 | tf_op jit(solution)/shard_map/all_gather | solution.py:65
  303.6 4.9 %multiply_reduce_fusion = (f32[]{:T(128)}, bf16[256,512]{0,1:T(8,128)(2,1)}, f32[]{:T(128)}) fusion(s32[512]{0:T(512)S(1)} %iota_add_fusion, s32[256]{0:T(256)S(1)} %iota_add_fusion.1, bf16[256,512]{0,1:T(8,128)(2,1)S(1)} %copy-done, f32[]{:T(128)S(6)} %convert_element_type.61, bf16[4096,512]{1,0:T(8,128)(2,1)} %all-gather.15.cloned.1.call-done, ...), kind=kOutput, calls=%fused_computation.31 | convolution fusion | flops 1075314688 | bytes 6818828 | tf_op jit(solution)/shard_map/dot_general | solution.py:67
  308.7 1.5 broadcast_in_dim.8
  310.2 5.3 %all-to-all-start.2 = ((bf16[8,256,512]{1,2,0:T(8,128)(2,1)}), bf16[8,256,512]{1,2,0:T(8,128)(2,1)S(1)}, u32[]{:S(2)}, u32[]{:S(2)}) async-start(bf16[8,256,512]{1,2,0:T(8,128)(2,1)} %broadcast_in_dim.8), calls=%async_computation.2 | async-start | bytes 4194304 | tf_op jit(solution)/shard_map/all_to_all | solution.py:28
  315.5 2.5 pad_maximum_fusion
  318.0 6.8 %psum.60 = f32[4]{0:T(128)S(1)} all-reduce(f32[4]{0:T(128)S(1)} %pad_maximum_fusion), channel_id=1, replica_groups=mesh['row_0'=4,'row_1'=4,'col_0'=4,'col_1'=2] {'row_0'}, use_global_device_ids=true, to_apply=%region_9.0 | all-reduce | flops 4 | bytes 32 | tf_op jit(solution)/shard_map/psum | solution.py:17
  324.9 7.2 %psum.61 = f32[4]{0:T(128)S(1)} all-reduce(f32[4]{0:T(128)S(1)} %psum.60), channel_id=1, replica_groups=mesh['row_0'=4,'row_1'=4,'col_0'=4,'col_1'=2] {'row_1'}, use_global_device_ids=true, to_apply=%region_10.0 | all-reduce | flops 4 | bytes 32 | tf_op jit(solution)/shard_map/psum | solution.py:17
  332.1 9.3 %psum.62 = f32[4]{0:T(128)S(1)} all-reduce(f32[4]{0:T(128)S(1)} %psum.61), channel_id=1, replica_groups=mesh['row_0'=4,'row_1'=4,'col_0'=4,'col_1'=2] {'col_0'}, use_global_device_ids=true, to_apply=%region_11.0 | all-reduce | flops 4 | bytes 32 | tf_op jit(solution)/shard_map/psum | solution.py:17
  341.4 5.1 %psum.63 = f32[4]{0:T(128)S(1)} all-reduce(f32[4]{0:T(128)S(1)} %psum.62), channel_id=1, replica_groups=mesh['row_0'=4,'row_1'=4,'col_0'=4,'col_1'=2] {'col_1'}, use_global_device_ids=true, to_apply=%region_12.0 | all-reduce | flops 4 | bytes 32 | tf_op jit(solution)/shard_map/psum | solution.py:17
  346.4 0.5 multiply_sqrt_fusion
  347.0 16.8 %all-gather.17.cloned.1.call-done = bf16[4096,512]{0,1:T(8,128)(2,1)} async-done(((bf16[256,512]{0,1:T(8,128)(2,1)}), bf16[4096,512]{0,1:T(8,128)(2,1)}) %all-gather.17.cloned.1.call-update) | async-done | bytes 4194320 | tf_op jit(solution)/shard_map/all_gather | solution.py:73
  363.8 4.3 %fusion.17 = f32[256,512]{1,0:T(8,128)} fusion(bf16[256,4096]{0,1:T(8,128)(2,1)S(1)} %bitcast.39, bf16[4096,512]{0,1:T(8,128)(2,1)} %all-gather.17.cloned.1.call-done), kind=kOutput, calls=%fused_computation.39 | convolution fusion | flops 1073741824 | bytes 6815744 | tf_op jit(solution)/shard_map/dot_general | solution.py:71
  (28 shorter events, 0.6 us)
Async XLA Ops:
  7.2 9.7 %copy-start.1 = (f32[256,512]{1,0:T(8,128)S(1)}, f32[256,512]{1,0:T(8,128)}, u32[]{:S(2)}) copy-start(f32[256,512]{1,0:T(8,128)} %param.1) | copy-start | bytes 1572868
  7.2 59.1 %all-gather.7.cloned.1.call-start = ((), (), s32[]{:S(2)}) async-start(), calls=%async_computation.3 | async-start | bytes 4456448 | tf_op jit(solution)/shard_map/all_gather | solution.py:51
  11.8 37.0 %all-to-all-start = ((bf16[8,256,512]{2,1,0:T(8,128)(2,1)}), bf16[8,256,512]{2,1,0:T(8,128)(2,1)S(1)}, u32[]{:S(2)}, u32[]{:S(2)}) async-start(bf16[8,256,512]{2,1,0:T(8,128)(2,1)} %broadcast_in_dim.6), calls=%async_computation | async-start | bytes 4194304 | tf_op jit(solution)/shard_map/all_to_all | solution.py:28
  16.9 112.6 %all-gather.9.cloned.1.call-start = ((), (), s32[]{:S(2)}) async-start(), calls=%async_computation.4 | async-start | bytes 4456448 | tf_op jit(solution)/shard_map/all_gather | solution.py:73
  66.3 63.2 %copy-start.2 = (bf16[8,256,512]{1,2,0:T(8,128)(2,1)S(1)}, bf16[8,256,512]{1,2,0:T(8,128)(2,1)}, u32[]{:S(2)}) copy-start(bf16[8,256,512]{1,2,0:T(8,128)(2,1)} %copy.15) | copy-start | bytes 6291460
  73.1 113.2 %all-gather.11.cloned.1.call-start = ((), (), s32[]{:S(2)}) async-start(), calls=%async_computation.5 | async-start | bytes 4456448 | tf_op jit(solution)/shard_map/all_gather | solution.py:65
  133.9 57.3 %copy-start.4 = (bf16[256,512]{1,0:T(8,128)(2,1)S(1)}, bf16[256,512]{1,0:T(8,128)(2,1)}, u32[]{:S(2)}) copy-start(bf16[256,512]{1,0:T(8,128)(2,1)} %fusion.11) | copy-start | bytes 786436
  133.9 112.4 %all-gather.13.cloned.1.call-start = ((), (), s32[]{:S(2)}) async-start(), calls=%async_computation.6 | async-start | bytes 4456448 | tf_op jit(solution)/shard_map/all_gather | solution.py:73
  191.2 112.5 %all-gather.15.cloned.1.call-start = ((), (), s32[]{:S(2)}) async-start(), calls=%async_computation.7 | async-start | bytes 4456448 | tf_op jit(solution)/shard_map/all_gather | solution.py:65
  222.0 81.6 %copy-start = (bf16[256,512]{0,1:T(8,128)(2,1)S(1)}, bf16[256,512]{0,1:T(8,128)(2,1)}, u32[]{:S(2)}) copy-start(bf16[256,512]{0,1:T(8,128)(2,1)} %copy.13) | copy-start | bytes 786436
  251.2 57.4 %copy-start.3 = (bf16[256,512]{1,0:T(8,128)(2,1)S(1)}, bf16[256,512]{1,0:T(8,128)(2,1)}, u32[]{:S(2)}) copy-start(bf16[256,512]{1,0:T(8,128)(2,1)} %convolution_convert_fusion) | copy-start | bytes 786436
  251.2 112.6 %all-gather.17.cloned.1.call-start = ((), (), s32[]{:S(2)}) async-start(), calls=%async_computation.8 | async-start | bytes 4456448 | tf_op jit(solution)/shard_map/all_gather | solution.py:73
  310.2 36.8 %all-to-all-start.2 = ((bf16[8,256,512]{1,2,0:T(8,128)(2,1)}), bf16[8,256,512]{1,2,0:T(8,128)(2,1)S(1)}, u32[]{:S(2)}, u32[]{:S(2)}) async-start(bf16[8,256,512]{1,2,0:T(8,128)(2,1)} %broadcast_in_dim.8), calls=%async_computation.2 | async-start | bytes 4194304 | tf_op jit(solution)/shard_map/all_to_all | solution.py:28
Sparse Core Ops, SparseCore 0:
  10.7 55.5 all-gather.6
  73.2 56.1 all-gather.8
  134.0 52.2 all-gather.10
  191.3 55.0 all-gather.12
  251.3 52.2 all-gather.14
  308.7 55.0 all-gather.16
